TPU v7x, 512 devices: a whole 4x4x16 slice. The times are simulated.
512 devices in a mesh: grp: 64 (over z, x_lo, core), tp: 8 (over x_hi, y).
Axes of the slice: x: 4 (x_hi: 2, x_lo: 2; x = x_hi * 2 + x_lo), y: 4, z: 16, core: 2. Of those that a mesh axis runs over, the one named last changes fastest.
Arguments:
- memory_rows: bfloat16 [65536, 4096], P('grp', 'tp'), may hold values from -24 to 24, as said below
- norm_gain: float32 [4096], replicated, may hold values from 0.25 to 1.75
- key_weight: bfloat16 [4096, 4096], P(None, 'tp'), may hold values from -0.09375 to 0.09375
- owner_table: int32 [8192], replicated, may hold values from 0 to 8191, as said below
Outputs:
- placed_keys: bfloat16 [65536, 4096], P('grp', 'tp')
Inputs may be any that keep to these rules, and one draw needn't show every extreme that they name: A permutation of the 8192 block numbers. Block b of the input goes to block position owner_table[b], which lies in group owner_table[b] // 128. The 128 blocks of one group go to all 64 groups, exactly 2 blocks to each of them. `memory_rows`: rows have offsets and scales of their own, and features a common pattern.
All inputs are finite; a program needn't handle non-finite values.
Results may differ from a plain program's by a relative error of at most 0.0049.
Values may be sent and summed in bfloat16 or wider, within the bound.
No kernel may reach another device: no remote copies, remote signals or barrier semaphores. Data moves between devices by JAX's collectives and lax.ppermute only.
A program may use at most 64 MiB of HBM per device.

v0:
```python
import jax
import jax.numpy as jnp
from jax import lax
from jax.sharding import PartitionSpec as P

BLK_ROWS = 8
EPS = 1e-05


def to_owners(block_rows, owner_table):
    groups = lax.axis_size("grp")
    position = lax.axis_index("grp")
    row_count, col_count = block_rows.shape
    blocks_here = row_count // BLK_ROWS
    capacity = max(1, blocks_here // groups)
    owned_slots = lax.dynamic_slice_in_dim(owner_table, position * blocks_here, blocks_here)
    target = owned_slots // blocks_here
    block_ids = jnp.arange(blocks_here, dtype=jnp.int32)
    earlier = (target[None, :] == target[:, None]) & (block_ids[None, :] < block_ids[:, None])
    rank = jnp.sum(earlier.astype(jnp.int32), axis=1)
    send_slot = target * capacity + rank
    slot_ids = jnp.arange(groups * capacity, dtype=jnp.int32)
    sender = (send_slot[None, :] == slot_ids[:, None]).astype(jnp.bfloat16)
    flattened = block_rows.reshape(blocks_here, BLK_ROWS * col_count)
    outgoing = jnp.dot(sender, flattened, preferred_element_type=jnp.float32).astype(jnp.bfloat16)
    incoming = lax.all_to_all(outgoing, "grp", split_axis=0, concat_axis=0, tiled=True)
    block_total = owner_table.shape[0]
    inverse = (
        jnp.zeros((block_total,), jnp.int32)
        .at[owner_table]
        .set(jnp.arange(block_total, dtype=jnp.int32))
    )
    arriving = lax.dynamic_slice_in_dim(inverse, position * blocks_here, blocks_here)
    anchor_group = arriving // blocks_here
    anchor_column = arriving % blocks_here
    target_table = owner_table.reshape(groups, blocks_here) // blocks_here
    anchor_targets = target_table[anchor_group]
    before = (anchor_targets == position) & (block_ids[None, :] < anchor_column[:, None])
    anchor_rank = jnp.sum(before.astype(jnp.int32), axis=1)
    source_slot = anchor_group * capacity + anchor_rank
    picker = (source_slot[:, None] == slot_ids[None, :]).astype(jnp.bfloat16)
    placed = jnp.dot(picker, incoming, preferred_element_type=jnp.float32).astype(jnp.bfloat16)
    return placed.reshape(row_count, col_count)


def project(memory_rows, norm_gain, key_weight):
    width = norm_gain.shape[0]
    whole_rows = lax.all_gather(memory_rows, "tp", axis=1, tiled=True)
    values = whole_rows.astype(jnp.float32)
    row_mean = jnp.sum(values, axis=1, keepdims=True) / width
    row_var = jnp.sum(values * values, axis=1, keepdims=True) / width - row_mean * row_mean
    normed = ((values - row_mean) * lax.rsqrt(row_var + EPS) * norm_gain[None, :]).astype(
        jnp.bfloat16
    )
    keys = jnp.dot(normed, key_weight, preferred_element_type=jnp.float32)
    return keys.astype(jnp.bfloat16)


def on_device(memory_rows, norm_gain, key_weight, owner_table):
    keys = project(memory_rows, norm_gain, key_weight)
    return to_owners(keys, owner_table)


def solution(mesh):
    in_specs = (P("grp", "tp"), P(), P(None, "tp"), P())
    out_specs = P("grp", "tp")
    return jax.shard_map(
        on_device, mesh=mesh, in_specs=in_specs, out_specs=out_specs, check_vma=False
    )
```

profile of v0, /device:TPU:2, one launch (start us, length us, event | category | flops | bytes accessed | tf_op | source)
XLA Modules:
  0.0 236.6 jit_solution(608830909230115830)
XLA Ops:
  6.5 0.0 copy-start.2
  6.5 0.0 all-gather.2.cloned.1.call-start
  6.5 0.7 all-gather.2.cloned.1.call-update
  7.3 0.8 and_select_fusion
  8.0 0.2 convert_reduce_fusion.1
  8.2 0.8 multiply_add_fusion
  9.0 132.8 %all-gather.2.cloned.1.call-done = bf16[1024,4096]{1,0:T(8,128)(2,1)} async-done(((bf16[1024,512]{1,0:T(8,128)(2,1)}), bf16[1024,4096]{1,0:T(8,128)(2,1)}) %all-gather.2.cloned.1.call-update) | async-done | bytes 8388624 | tf_op jit(solution)/shard_map/all_gather | solution.py:48
  141.8 0.0 copy-start
  141.8 6.1 %convert_reduce_fusion = (f32[1024]{0:T(1024)S(1)}, f32[1024]{0:T(1024)S(1)}) fusion(bf16[1024,4096]{1,0:T(8,128)(2,1)} %all-gather.2.cloned.1.call-done), kind=kLoop, calls=%fused_computation.4 | loop fusion | flops 16775168 | bytes 8396800 | tf_op jit(solution)/shard_map/reduce_sum | solution.py:50
  147.9 0.0 copy-done.2
  147.9 0.0 copy-done
  147.9 6.8 %fusion.9 = bf16[1024,512]{1,0:T(8,128)(2,1)S(1)} fusion(bf16[4096,512]{1,0:T(8,128)(2,1)} %param.6, bf16[1024,4096]{1,0:T(8,128)(2,1)S(1)} %copy-done, f32[4096]{0:T(1024)S(1)} %copy-done.2, f32[1024]{0:T(1024)S(1)} %get-tuple-element.12, f32[1024]{0:T(1024)S(1)} %get-tuple-element.11), kind=kOutput, calls=%fused_computation.15 | convolution fusion | flops 4316463104 | bytes 13656064 | tf_op jit(solution)/shard_map/dot_general | solution.py:55
  154.8 0.0 copy-start.1
  154.8 0.5 reshape.36
  155.3 0.4 convolution_convert_fusion.1
  155.8 1.5 all_to_all.8
  157.3 14.2 %all-to-all-start = ((bf16[64,2,4096]{2,1,0:T(2,128)(2,1)}), bf16[64,2,4096]{2,1,0:T(2,128)(2,1)S(1)}, u32[]{:S(2)}, u32[]{:S(2)}) async-start(bf16[64,2,4096]{2,1,0:T(2,128)(2,1)} %all_to_all.8), calls=%async_computation | async-start | bytes 2097152 | tf_op jit(solution)/shard_map/all_to_all | solution.py:26
  171.5 0.0 copy-done.1
  171.5 30.5 %scatter_custom_fusion = s32[8192]{0:T(1024)S(1)} fusion(s32[8192]{0:T(1024)S(1)} %compare_select_fusion, s32[8192]{0:T(1024)S(1)} %iota.11, s32[]{:T(128)} %constant.54.clone.1), kind=kCustom, calls=%fused_computation.36 | custom fusion | bytes 32772 | tf_op jit(solution)/shard_map/scatter | solution.py:31
  202.0 0.1 and_select_fusion.1
  202.1 0.1 compare_select_fusion.1
  202.2 0.6 gather_fusion
  202.8 0.2 convert_reduce_fusion.2
  203.0 24.5 %all-to-all-done = bf16[64,2,4096]{2,1,0:T(2,128)(2,1)S(1)} async-done(((bf16[64,2,4096]{2,1,0:T(2,128)(2,1)}), bf16[64,2,4096]{2,1,0:T(2,128)(2,1)S(1)}, u32[]{:S(2)}, u32[]{:S(2)}) %all-to-all-start) | async-done | bytes 1048608 | tf_op jit(solution)/shard_map/all_to_all | solution.py:26
  227.5 0.4 all_to_all.10
  227.9 0.5 convolution_convert_fusion
  228.4 1.3 reshape.37
  (6 shorter events, 0.1 us)
Async XLA Ops:
  6.5 141.4 %copy-start.2 = (f32[4096]{0:T(1024)S(1)}, f32[4096]{0:T(1024)}, u32[]{:S(2)}) copy-start(f32[4096]{0:T(1024)} %param.5) | copy-start | bytes 49156
  6.5 135.3 %all-gather.2.cloned.1.call-start = ((), (), s32[]{:S(2)}) async-start(), calls=%async_computation.1 | async-start | bytes 9437184 | tf_op jit(solution)/shard_map/all_gather | solution.py:48
  141.8 6.1 %copy-start = (bf16[1024,4096]{1,0:T(8,128)(2,1)S(1)}, bf16[1024,4096]{1,0:T(8,128)(2,1)}, u32[]{:S(2)}) copy-start(bf16[1024,4096]{1,0:T(8,128)(2,1)} %all-gather.2.cloned.1.call-done) | copy-start | bytes 25165828
  154.8 16.7 %copy-start.1 = (s32[8192]{0:T(1024)S(1)}, s32[8192]{0:T(1024)}, u32[]{:S(2)}) copy-start(s32[8192]{0:T(1024)} %param.7) | copy-start | bytes 98308
  157.3 70.2 %all-to-all-start = ((bf16[64,2,4096]{2,1,0:T(2,128)(2,1)}), bf16[64,2,4096]{2,1,0:T(2,128)(2,1)S(1)}, u32[]{:S(2)}, u32[]{:S(2)}) async-start(bf16[64,2,4096]{2,1,0:T(2,128)(2,1)} %all_to_all.8), calls=%async_computation | async-start | bytes 2097152 | tf_op jit(solution)/shard_map/all_to_all | solution.py:26
Sparse Core Ops, SparseCore 0:
  10.4 131.3 all-gather.1
where the time goes:
time: 237 us
  waiting for transfers between devices  158 us (67%)
  local copies, waits for them, and re-layouts  34.9 us (15%)
  starting transfers between devices  14.2 us (6%)
  between operations  13.5 us (6%)
  other arithmetic  8.2 us (3%)
  matrix products  7.75 us (3%)
    all_gather x1, waiting for transfers between devices, project(): whole_rows = lax.all_gather(memory_rows, 'tp', axis=1, tiled=True)  133 us
    scatter x1, local copies, waits for them, and re-layouts, to_owners(): inverse = jnp.zeros((block_total,), jnp.int32).at[owner_table].set(jnp.ar...  30.5 us
    all_to_all x1, waiting for transfers between devices, to_owners(): lax.all_to_all(outgoing, 'grp', split_axis=0, concat_axis=0, tiled=True)  24.5 us
    all_to_all x1, starting transfers between devices, to_owners(): lax.all_to_all(outgoing, 'grp', split_axis=0, concat_axis=0, tiled=True)  14.2 us
    dot_general x1, matrix products, project(): keys = jnp.dot(normed, key_weight, preferred_element_type=jnp.float32)  6.84 us
    reduce_sum x1, other arithmetic, project(): row_mean = jnp.sum(values, axis=1, keepdims=True) / width  6.09 us
  transfers between devices with their start and end apart: 2, of which 2 were waited for; matrix products, arithmetic and copies ran while one was open for 14% of the time, Pallas kernels for 0%

commit v1 on v0

--- a/solution.py
+++ b/solution.py
@@ -45,7 +45,9 @@
 
 def project(memory_rows, norm_gain, key_weight):
     width = norm_gain.shape[0]
-    whole_rows = lax.all_gather(memory_rows, "tp", axis=1, tiled=True)
+    whole_rows = jnp.concatenate(
+        lax.all_to_all(jnp.stack([memory_rows] * lax.axis_size("tp")), "tp", 0, 0), axis=1
+    )
     values = whole_rows.astype(jnp.float32)
     row_mean = jnp.sum(values, axis=1, keepdims=True) / width
     row_var = jnp.sum(values * values, axis=1, keepdims=True) / width - row_mean * row_mean

time: 237 us -> 200 us (0.84)
  the two profiles are of different devices: /device:TPU:2 before, /device:TPU:6 now
where the time goes in v1:
time: 200 us
  waiting for transfers between devices  117 us (58%)
  local copies, waits for them, and re-layouts  40.7 us (20%)
  starting transfers between devices  24.7 us (12%)
  other arithmetic  11.8 us (6%)
  matrix products  5.42 us (3%)
    all_to_all x1, waiting for transfers between devices, project(): lax.all_to_all(jnp.stack([memory_rows] * lax.axis_size('tp')), 'tp', 0, 0)  92.6 us
    scatter x1, local copies, waits for them, and re-layouts, to_owners(): inverse = jnp.zeros((block_total,), jnp.int32).at[owner_table].set(jnp.ar...  30.5 us
    all_to_all x1, waiting for transfers between devices, to_owners(): lax.all_to_all(outgoing, 'grp', split_axis=0, concat_axis=0, tiled=True)  24.5 us
    all_to_all x1, starting transfers between devices, to_owners(): lax.all_to_all(outgoing, 'grp', split_axis=0, concat_axis=0, tiled=True)  17.1 us
    all_to_all x1, starting transfers between devices, project(): lax.all_to_all(jnp.stack([memory_rows] * lax.axis_size('tp')), 'tp', 0, 0)  7.57 us
    reduce_sum x1, other arithmetic, project(): row_mean = jnp.sum(values, axis=1, keepdims=True) / width  5.6 us
    convert_element_type x1, other arithmetic, project(): ((values - row_mean) * lax.rsqrt(row_var + EPS) * norm_gain[None, :]).ast...  5.51 us
    dot_general x1, matrix products, project(): keys = jnp.dot(normed, key_weight, preferred_element_type=jnp.float32)  4.52 us
  transfers between devices with their start and end apart: 2, of which 2 were waited for; matrix products, arithmetic and copies ran while one was open for 16% of the time, Pallas kernels for 0%

profile of v1, /device:TPU:6, one launch (start us, length us, event | category | flops | bytes accessed | tf_op | source)
XLA Modules:
  0.0 199.9 jit_solution(9420855359398352423)
XLA Ops:
  0.0 1.5 copy.6
  1.5 4.3 %stack.2 = bf16[8,1024,512]{1,2,0:T(8,128)(2,1)} broadcast(bf16[1024,512]{0,1:T(8,128)(2,1)S(1)} %copy.6), dimensions={1,2} | broadcast | bytes 9437184 | tf_op jit(solution)/shard_map/stack | solution.py:49
  5.8 0.0 copy-start
  5.8 7.6 %all-to-all-start = ((bf16[8,1024,512]{1,2,0:T(8,128)(2,1)}), bf16[8,1024,512]{1,2,0:T(8,128)(2,1)}, u32[]{:S(2)}, u32[]{:S(2)}) async-start(bf16[8,1024,512]{1,2,0:T(8,128)(2,1)} %stack.2), calls=%async_computation | async-start | bytes 16777216 | tf_op jit(solution)/shard_map/all_to_all | solution.py:49
  13.4 0.0 copy-start.1
  13.4 0.0 copy-done
  13.4 0.1 and_select_fusion
  13.4 0.2 convert_reduce_fusion.1
  13.6 0.1 multiply_add_fusion
  13.7 92.6 %all-to-all-done = bf16[8,1024,512]{1,2,0:T(8,128)(2,1)} async-done(((bf16[8,1024,512]{1,2,0:T(8,128)(2,1)}), bf16[8,1024,512]{1,2,0:T(8,128)(2,1)}, u32[]{:S(2)}, u32[]{:S(2)}) %all-to-all-start) | async-done | bytes 8388640 | tf_op jit(solution)/shard_map/all_to_all | solution.py:49
  106.3 5.6 %convert_reduce_fusion = (f32[1024]{0:T(1024)S(1)}, f32[1024]{0:T(1024)S(1)}) fusion(bf16[8,1024,512]{1,2,0:T(8,128)(2,1)} %all-to-all-done), kind=kLoop, calls=%fused_computation.7 | loop fusion | flops 16775168 | bytes 8396800 | tf_op jit(solution)/shard_map/reduce_sum | solution.py:52
  112.0 0.0 copy-done.1
  112.0 0.0 copy-start.2
  112.0 5.5 %fusion.2 = bf16[1024,4096]{0,1:T(8,128)(2,1)S(1)} fusion(bf16[8,1024,512]{1,2,0:T(8,128)(2,1)} %all-to-all-done, f32[4096]{0:T(1024)S(1)} %copy-done.1, f32[1024]{0:T(1024)S(1)} %get-tuple-element.12, f32[1024]{0:T(1024)S(1)} %get-tuple-element.11), kind=kLoop, calls=%fused_computation.5 | loop fusion | flops 20971520 | bytes 16801792 | tf_op jit(solution)/shard_map/convert_element_type | solution.py:54
  117.5 0.0 copy-done.2
  117.5 4.5 %convolution_convert_fusion.2 = bf16[1024,512]{1,0:T(8,128)(2,1)S(1)} fusion(bf16[1024,4096]{0,1:T(8,128)(2,1)S(1)} %fusion.2, bf16[4096,512]{1,0:T(8,128)(2,1)S(1)} %copy-done.2), kind=kOutput, calls=%fused_computation.10 | convolution fusion | flops 4295491584 | bytes 13631488 | tf_op jit(solution)/shard_map/dot_general | solution.py:57
  122.0 0.5 reshape.42
  122.6 0.4 convolution_convert_fusion.1
  123.0 1.5 all_to_all.12
  124.5 17.1 %all-to-all-start.1 = ((bf16[64,2,4096]{2,1,0:T(2,128)(2,1)}), bf16[64,2,4096]{2,1,0:T(2,128)(2,1)S(1)}, u32[]{:S(2)}, u32[]{:S(2)}) async-start(bf16[64,2,4096]{2,1,0:T(2,128)(2,1)} %all_to_all.12), calls=%async_computation.1 | async-start | bytes 2097152 | tf_op jit(solution)/shard_map/all_to_all | solution.py:26
  141.6 30.5 %scatter_custom_fusion = s32[8192]{0:T(1024)S(1)} fusion(s32[8192]{0:T(1024)S(1)} %compare_select_fusion, s32[8192]{0:T(1024)S(1)} %iota.11, s32[]{:T(128)} %constant.54.clone.1), kind=kCustom, calls=%fused_computation.31 | custom fusion | bytes 32772 | tf_op jit(solution)/shard_map/scatter | solution.py:31
  172.1 0.1 and_select_fusion.1
  172.2 0.1 compare_select_fusion.1
  172.3 0.6 gather_fusion
  173.0 0.2 convert_reduce_fusion.2
  173.2 24.5 %all-to-all-done.1 = bf16[64,2,4096]{2,1,0:T(2,128)(2,1)S(1)} async-done(((bf16[64,2,4096]{2,1,0:T(2,128)(2,1)}), bf16[64,2,4096]{2,1,0:T(2,128)(2,1)S(1)}, u32[]{:S(2)}, u32[]{:S(2)}) %all-to-all-start.1) | async-done | bytes 1048608 | tf_op jit(solution)/shard_map/all_to_all | solution.py:26
  197.7 0.4 all_to_all.14
  198.1 0.5 convolution_convert_fusion
  198.6 1.3 reshape.43
  (6 shorter events, 0.1 us)
Async XLA Ops:
  5.8 7.6 %copy-start = (s32[8192]{0:T(1024)S(1)}, s32[8192]{0:T(1024)}, u32[]{:S(2)}) copy-start(s32[8192]{0:T(1024)} %param.7) | copy-start | bytes 98308
  5.8 100.6 %all-to-all-start = ((bf16[8,1024,512]{1,2,0:T(8,128)(2,1)}), bf16[8,1024,512]{1,2,0:T(8,128)(2,1)}, u32[]{:S(2)}, u32[]{:S(2)}) async-start(bf16[8,1024,512]{1,2,0:T(8,128)(2,1)} %stack.2), calls=%async_computation | async-start | bytes 16777216 | tf_op jit(solution)/shard_map/all_to_all | solution.py:49
  13.4 98.6 %copy-start.1 = (f32[4096]{0:T(1024)S(1)}, f32[4096]{0:T(1024)}, u32[]{:S(2)}) copy-start(f32[4096]{0:T(1024)} %param.5) | copy-start | bytes 49156
  112.0 5.5 %copy-start.2 = (bf16[4096,512]{1,0:T(8,128)(2,1)S(1)}, bf16[4096,512]{1,0:T(8,128)(2,1)}, u32[]{:S(2)}) copy-start(bf16[4096,512]{1,0:T(8,128)(2,1)} %param.6) | copy-start | bytes 12582916
  124.5 73.2 %all-to-all-start.1 = ((bf16[64,2,4096]{2,1,0:T(2,128)(2,1)}), bf16[64,2,4096]{2,1,0:T(2,128)(2,1)S(1)}, u32[]{:S(2)}, u32[]{:S(2)}) async-start(bf16[64,2,4096]{2,1,0:T(2,128)(2,1)} %all_to_all.12), calls=%async_computation.1 | async-start | bytes 2097152 | tf_op jit(solution)/shard_map/all_to_all | solution.py:26
